TPU v7x, 128 devices: a whole 4x4x4 slice. The times are simulated.
128 devices in a mesh: row: 8 (over x_lo, z), col: 16 (over y, x_hi, core).
Axes of the slice: x: 4 (x_hi: 2, x_lo: 2; x = x_hi * 2 + x_lo), y: 4, z: 4, core: 2. Of those that a mesh axis runs over, the one named last changes fastest.
Arguments:
- q_base: bfloat16 [8192, 8192], P('row', 'col'), may hold values from -600 to 600
- q_down: bfloat16 [64, 8192], P(None, 'col'), may hold values from -1.1953125 to 1.1953125
- q_up: bfloat16 [8192, 64], P('row'), may hold values from -1.1953125 to 1.1953125
- q_magnitude: float32 [8192], P('row'), may hold values from 40 to 200
- k_base: bfloat16 [1024, 8192], P('row', 'col'), may hold values from -600 to 600
- k_down: bfloat16 [64, 8192], P(None, 'col'), may hold values from -1.1953125 to 1.1953125
- k_up: bfloat16 [1024, 64], P('row'), may hold values from -1.1953125 to 1.1953125
- k_magnitude: float32 [1024], P('row'), may hold values from 40 to 200
- v_base: bfloat16 [1024, 8192], P('row', 'col'), may hold values from -600 to 600
- v_down: bfloat16 [64, 8192], P(None, 'col'), may hold values from -1.1953125 to 1.1953125
- v_up: bfloat16 [1024, 64], P('row'), may hold values from -1.1953125 to 1.1953125
- v_magnitude: float32 [1024], P('row'), may hold values from 40 to 200
- o_base: bfloat16 [8192, 8192], P('row', 'col'), may hold values from -600 to 600
- o_down: bfloat16 [64, 8192], P(None, 'col'), may hold values from -1.1953125 to 1.1953125
- o_up: bfloat16 [8192, 64], P('row'), may hold values from -1.1953125 to 1.1953125
- o_magnitude: float32 [8192], P('row'), may hold values from 40 to 200
- gate_base: bfloat16 [29568, 8192], P('row', 'col'), may hold values from -600 to 600
- gate_down: bfloat16 [64, 8192], P(None, 'col'), may hold values from -1.1953125 to 1.1953125
- gate_up: bfloat16 [29568, 64], P('row'), may hold values from -1.1953125 to 1.1953125
- gate_magnitude: float32 [29568], P('row'), may hold values from 40 to 200
- lift_base: bfloat16 [29568, 8192], P('row', 'col'), may hold values from -600 to 600
- lift_down: bfloat16 [64, 8192], P(None, 'col'), may hold values from -1.1953125 to 1.1953125
- lift_up: bfloat16 [29568, 64], P('row'), may hold values from -1.1953125 to 1.1953125
- lift_magnitude: float32 [29568], P('row'), may hold values from 40 to 200
Outputs:
- q_merged: bfloat16 [8192, 8192], P(('row', 'col'))
- k_merged: bfloat16 [1024, 8192], P(('row', 'col'))
- v_merged: bfloat16 [1024, 8192], P(('row', 'col'))
- o_merged: bfloat16 [8192, 8192], P(None, ('col', 'row'))
- gate_merged: bfloat16 [29568, 8192], P(('row', 'col'))
- lift_merged: bfloat16 [29568, 8192], P(('row', 'col'))
All inputs are finite; a program needn't handle non-finite values.
Results may differ from a plain program's by a relative error of at most 0.001.
Values may be sent and summed in bfloat16 or wider, within the bound.
A program may use at most 128 MiB of HBM per device.

v0:
```python
import jax
import jax.numpy as jnp
from jax import lax
from jax.sharding import Mesh
from jax.sharding import PartitionSpec as P

COL = ("col_0", "col_1", "col_2")
ROW_COL = ("row", "col_0", "col_1", "col_2")
COL_ROW = ("col_0", "col_1", "col_2", "row")
eps = 1e-06


def over_axes(value, axes):
    for axis in axes:
        value = lax.psum(value, axis)
    return value


def tile_merge(base, down, up, magnitude):
    direction = base.astype(jnp.float32) + jnp.dot(up, down, preferred_element_type=jnp.float32)
    partial_sum = jnp.sum(direction * direction, axis=1)
    total = over_axes(partial_sum, COL)
    factor = magnitude * lax.rsqrt(total + eps)
    return (direction * factor[:, None]).astype(jnp.bfloat16)


def row_split(base, down, up, magnitude):
    merged = tile_merge(base, down, up, magnitude)
    return lax.all_to_all(merged, COL, split_axis=0, concat_axis=1, tiled=True)


def on_device(
    q_base,
    q_down,
    q_up,
    q_magnitude,
    k_base,
    k_down,
    k_up,
    k_magnitude,
    v_base,
    v_down,
    v_up,
    v_magnitude,
    o_base,
    o_down,
    o_up,
    o_magnitude,
    gate_base,
    gate_down,
    gate_up,
    gate_magnitude,
    lift_base,
    lift_down,
    lift_up,
    lift_magnitude,
):
    q_merged = row_split(q_base, q_down, q_up, q_magnitude)
    k_merged = row_split(k_base, k_down, k_up, k_magnitude)
    v_merged = row_split(v_base, v_down, v_up, v_magnitude)
    o_tile = tile_merge(o_base, o_down, o_up, o_magnitude)
    o_merged = lax.all_to_all(o_tile, "row", split_axis=1, concat_axis=0, tiled=True)
    gate_merged = row_split(gate_base, gate_down, gate_up, gate_magnitude)
    lift_merged = row_split(lift_base, lift_down, lift_up, lift_magnitude)
    return (q_merged, k_merged, v_merged, o_merged, gate_merged, lift_merged)


def solution(mesh):
    finer = Mesh(
        mesh.devices.reshape(mesh.shape["row"], 4, 2, 2), ("row", "col_0", "col_1", "col_2")
    )
    placed = (
        P("row", COL),
        P(None, COL),
        P("row", None),
        P("row"),
        P("row", COL),
        P(None, COL),
        P("row", None),
        P("row"),
        P("row", COL),
        P(None, COL),
        P("row", None),
        P("row"),
        P("row", COL),
        P(None, COL),
        P("row", None),
        P("row"),
        P("row", COL),
        P(None, COL),
        P("row", None),
        P("row"),
        P("row", COL),
        P(None, COL),
        P("row", None),
        P("row"),
    )
    return jax.shard_map(
        on_device,
        mesh=finer,
        in_specs=placed,
        out_specs=(
            P(ROW_COL, None),
            P(ROW_COL, None),
            P(ROW_COL, None),
            P(None, COL_ROW),
            P(ROW_COL, None),
            P(ROW_COL, None),
        ),
        check_vma=False,
    )
```

profile of v0, /device:TPU:1, one launch (start us, length us, event | category | flops | bytes accessed | tf_op | source)
XLA Modules:
  0.0 232.9 jit_solution(16911114155286947436)
XLA Ops:
  0.6 0.0 copy-start
  0.7 1.5 copy.39
  2.2 0.0 copy-start.2
  2.2 0.0 copy-start.6
  2.2 1.4 multiply_reduce_fusion.5
  3.6 1.3 multiply_reduce_fusion.4
  4.9 2.7 %multiply_reduce_fusion.2 = (f32[1024]{0:T(1024)S(1)}, f32[1024,512]{0,1:T(8,128)}) fusion(bf16[1024,64]{0,1:T(8,128)(2,1)} %param.38, bf16[64,512]{1,0:T(8,128)(2,1)} %param.37, bf16[1024,512]{0,1:T(8,128)(2,1)S(1)} %copy.39), kind=kOutput, calls=%fused_computation.7 | convolution fusion | flops 69204992 | bytes 3346432 | tf_op jit(solution)/shard_map/dot_general | solution.py:20
  7.6 1.8 multiply_reduce_fusion.3
  9.4 0.0 copy-start.3
  9.4 0.0 copy-start.4
  9.5 0.0 copy-start.7
  9.5 4.3 %multiply_reduce_fusion.1 = (f32[3696]{0:T(1024)S(1)}, f32[3696,512]{1,0:T(8,128)}) fusion(bf16[3696,64]{0,1:T(8,128)(2,1)S(1)} %copy-done, bf16[64,512]{1,0:T(8,128)(2,1)S(1)} %copy-done.6, bf16[3696,512]{1,0:T(8,128)(2,1)S(1)} %copy-done.2), kind=kOutput, calls=%fused_computation.4 | convolution fusion | flops 249786768 | bytes 11907520 | tf_op jit(solution)/shard_map/dot_general | solution.py:20
  13.8 0.0 copy-start.14
  13.8 0.0 copy-start.11
  13.8 4.4 %multiply_reduce_fusion = (f32[3696]{0:T(1024)S(1)}, f32[3696,512]{1,0:T(8,128)}) fusion(bf16[3696,64]{0,1:T(8,128)(2,1)S(1)} %copy-done.4, bf16[64,512]{1,0:T(8,128)(2,1)S(1)} %copy-done.7, bf16[3696,512]{1,0:T(8,128)(2,1)S(1)} %copy-done.3), kind=kOutput, calls=%fused_computation.1 | convolution fusion | flops 249786768 | bytes 11907520 | tf_op jit(solution)/shard_map/dot_general | solution.py:20
  18.2 14.8 %all-reduce = (f32[1024]{0:T(1024)S(1)}, f32[128]{0:T(128)S(1)}, f32[128]{0:T(128)S(1)}, f32[1024]{0:T(1024)S(1)}, f32[3696]{0:T(1024)S(1)}, /*index=5*/f32[3696]{0:T(1024)S(1)}) all-reduce(f32[1024]{0:T(1024)S(1)} %get-tuple-element.24, ...), channel_id=1, replica_groups=mesh['row'=8,'col_0'=4,'col_1'=2,'col_2'=2] {'col_0'}, use_global_device_ids=true, to_apply=%region_1.0 | all-reduce | flops 9696 | bytes 77568 | tf_op jit(solution)/shard_map/psum | solution.py:15
  33.0 9.6 %all-reduce.2 = (f32[1024]{0:T(1024)S(1)}, f32[128]{0:T(128)S(1)}, f32[128]{0:T(128)S(1)}, f32[1024]{0:T(1024)S(1)}, f32[3696]{0:T(1024)S(1)}, /*index=5*/f32[3696]{0:T(1024)S(1)}) all-reduce(f32[1024]{0:T(1024)S(1)} %get-tuple-element.6, ...), channel_id=1, replica_groups=mesh['row'=8,'col_0'=4,'col_1'=2,'col_2'=2] {'col_1'}, use_global_device_ids=true, to_apply=%region_2.0 | all-reduce | flops 9696 | bytes 77568 | tf_op jit(solution)/shard_map/psum | solution.py:15
  42.7 9.8 %all-reduce.1 = (f32[1024]{0:T(1024)S(1)}, f32[128]{0:T(128)S(1)}, f32[128]{0:T(128)S(1)}, f32[1024]{0:T(1024)S(1)}, f32[3696]{0:T(1024)S(1)}, /*index=5*/f32[3696]{0:T(1024)S(1)}) all-reduce(f32[1024]{0:T(1024)S(1)} %get-tuple-element.18, ...), channel_id=1, replica_groups=mesh['row'=8,'col_0'=4,'col_1'=2,'col_2'=2] {'col_2'}, use_global_device_ids=true, to_apply=%region_3.0 | all-reduce | flops 9696 | bytes 77568 | tf_op jit(solution)/shard_map/psum | solution.py:15
  52.5 0.7 fusion.1
  53.2 3.5 %all-to-all-start.2 = ((bf16[16,8,512]{2,1,0:T(8,128)(2,1)}), bf16[16,8,512]{2,1,0:T(8,128)(2,1)S(1)}, u32[]{:S(2)}, u32[]{:S(2)}) async-start(bf16[16,8,512]{2,1,0:T(8,128)(2,1)} %fusion.1), calls=%async_computation.2 | async-start | bytes 262144 | tf_op jit(solution)/shard_map/all_to_all | solution.py:29
  56.7 0.7 fusion
  57.5 6.9 %all-to-all-done.2 = bf16[16,8,512]{2,1,0:T(8,128)(2,1)S(1)} async-done(((bf16[16,8,512]{2,1,0:T(8,128)(2,1)}), bf16[16,8,512]{2,1,0:T(8,128)(2,1)S(1)}, u32[]{:S(2)}, u32[]{:S(2)}) %all-to-all-start.2) | async-done | bytes 131104 | tf_op jit(solution)/shard_map/all_to_all | solution.py:29
  64.4 4.0 %all-to-all-start.1 = ((bf16[16,8,512]{2,1,0:T(8,128)(2,1)}), bf16[16,8,512]{2,1,0:T(8,128)(2,1)S(1)}, u32[]{:S(2)}, u32[]{:S(2)}) async-start(bf16[16,8,512]{2,1,0:T(8,128)(2,1)} %fusion), calls=%async_computation.1 | async-start | bytes 262144 | tf_op jit(solution)/shard_map/all_to_all | solution.py:29
  68.4 2.8 %multiply_convert_fusion.2 = bf16[1024,512]{0,1:T(8,128)(2,1)} fusion(f32[1024,512]{0,1:T(8,128)} %get-tuple-element.31, f32[1024]{0:T(1024)S(1)} %get-tuple-element.38), kind=kLoop, calls=%fused_computation.6 | loop fusion | flops 1048576 | bytes 3149824 | tf_op jit(solution)/shard_map/convert_element_type | solution.py:24
  71.2 4.9 %all-to-all-done.1 = bf16[16,8,512]{2,1,0:T(8,128)(2,1)S(1)} async-done(((bf16[16,8,512]{2,1,0:T(8,128)(2,1)}), bf16[16,8,512]{2,1,0:T(8,128)(2,1)S(1)}, u32[]{:S(2)}, u32[]{:S(2)}) %all-to-all-start.1) | async-done | bytes 131104 | tf_op jit(solution)/shard_map/all_to_all | solution.py:29
  76.1 5.2 %all-to-all-start.3 = ((bf16[1024,8,64]{0,2,1:T(8,128)(2,1)}), bf16[1024,8,64]{0,2,1:T(8,128)(2,1)}, u32[]{:S(2)}, u32[]{:S(2)}) async-start(bf16[1024,8,64]{0,2,1:T(8,128)(2,1)} %bitcast.41), calls=%async_computation.3 | async-start | bytes 2097152 | tf_op jit(solution)/shard_map/all_to_all | solution.py:62
  81.3 1.2 multiply_convert_fusion.3
  82.5 14.0 %all-to-all-done.3 = bf16[1024,8,64]{0,2,1:T(8,128)(2,1)} async-done(((bf16[1024,8,64]{0,2,1:T(8,128)(2,1)}), bf16[1024,8,64]{0,2,1:T(8,128)(2,1)}, u32[]{:S(2)}, u32[]{:S(2)}) %all-to-all-start.3) | async-done | bytes 1048608 | tf_op jit(solution)/shard_map/all_to_all | solution.py:62
  96.5 4.1 %all-to-all-start = ((bf16[16,64,512]{2,1,0:T(8,128)(2,1)}), bf16[16,64,512]{2,1,0:T(8,128)(2,1)S(1)}, u32[]{:S(2)}, u32[]{:S(2)}) async-start(bf16[16,64,512]{2,1,0:T(8,128)(2,1)} %bitcast.42), calls=%async_computation | async-start | bytes 2097152 | tf_op jit(solution)/shard_map/all_to_all | solution.py:29
  100.7 5.3 %multiply_convert_fusion = bf16[3696,512]{1,0:T(8,128)(2,1)} fusion(f32[3696,512]{1,0:T(8,128)} %get-tuple-element.35, f32[3696]{0:T(1024)S(1)} %get-tuple-element.36), kind=kLoop, calls=%fused_computation | loop fusion | flops 3784704 | bytes 11368896 | tf_op jit(solution)/shard_map/convert_element_type | solution.py:24
  106.0 4.0 %all_to_all.104 = bf16[16,231,512]{2,1,0:T(8,128)(2,1)} reshape(bf16[3696,512]{1,0:T(8,128)(2,1)} %multiply_convert_fusion) | data formatting | bytes 7569408 | tf_op jit(solution)/shard_map/all_to_all | solution.py:29
  109.9 7.9 %all-to-all-done = bf16[16,64,512]{2,1,0:T(8,128)(2,1)S(1)} async-done(((bf16[16,64,512]{2,1,0:T(8,128)(2,1)}), bf16[16,64,512]{2,1,0:T(8,128)(2,1)S(1)}, u32[]{:S(2)}, u32[]{:S(2)}) %all-to-all-start) | async-done | bytes 1048608 | tf_op jit(solution)/shard_map/all_to_all | solution.py:29
  117.9 5.2 %all-to-all-start.5 = ((bf16[16,231,512]{2,1,0:T(8,128)(2,1)}), bf16[16,231,512]{2,1,0:T(8,128)(2,1)}, u32[]{:S(2)}, u32[]{:S(2)}) async-start(bf16[16,231,512]{2,1,0:T(8,128)(2,1)} %all_to_all.104), calls=%async_computation.5 | async-start | bytes 7602176 | tf_op jit(solution)/shard_map/all_to_all | solution.py:29
  123.1 5.3 %multiply_convert_fusion.1 = bf16[3696,512]{1,0:T(8,128)(2,1)} fusion(f32[3696,512]{1,0:T(8,128)} %get-tuple-element.33, f32[3696]{0:T(1024)S(1)} %get-tuple-element.37), kind=kLoop, calls=%fused_computation.3 | loop fusion | flops 3784704 | bytes 11368896 | tf_op jit(solution)/shard_map/convert_element_type | solution.py:24
  128.4 4.0 %all_to_all.100 = bf16[16,231,512]{2,1,0:T(8,128)(2,1)} reshape(bf16[3696,512]{1,0:T(8,128)(2,1)} %multiply_convert_fusion.1) | data formatting | bytes 7569408 | tf_op jit(solution)/shard_map/all_to_all | solution.py:29
  132.4 37.6 %all-to-all-done.5 = bf16[16,231,512]{2,1,0:T(8,128)(2,1)} async-done(((bf16[16,231,512]{2,1,0:T(8,128)(2,1)}), bf16[16,231,512]{2,1,0:T(8,128)(2,1)}, u32[]{:S(2)}, u32[]{:S(2)}) %all-to-all-start.5) | async-done | bytes 3784736 | tf_op jit(solution)/shard_map/all_to_all | solution.py:29
  169.9 5.3 %all-to-all-start.4 = ((bf16[16,231,512]{2,1,0:T(8,128)(2,1)}), bf16[16,231,512]{2,1,0:T(8,128)(2,1)}, u32[]{:S(2)}, u32[]{:S(2)}) async-start(bf16[16,231,512]{2,1,0:T(8,128)(2,1)} %all_to_all.100), calls=%async_computation.4 | async-start | bytes 7602176 | tf_op jit(solution)/shard_map/all_to_all | solution.py:29
  175.2 2.3 copy.44
  177.5 1.1 copy.43
  178.5 3.4 %copy.42 = bf16[231,16,512]{2,1,0:T(8,128)(2,1)S(1)} copy(bf16[231,16,512]{2,0,1:T(8,128)(2,1)} %bitcast.11) | data formatting | bytes 7569408 | tf_op jit(solution)/shard_map/all_to_all | solution.py:29
  181.9 0.4 pad.1
  182.3 5.8 %copy.46 = bf16[29,8,16,512]{3,1,2,0:T(8,128)(2,1)} copy(bf16[29,8,16,512]{3,2,1,0:T(8,128)(2,1)S(1)} %bitcast.39) | data formatting | bytes 7602176
  188.1 33.9 %all-to-all-done.4 = bf16[16,231,512]{2,1,0:T(8,128)(2,1)} async-done(((bf16[16,231,512]{2,1,0:T(8,128)(2,1)}), bf16[16,231,512]{2,1,0:T(8,128)(2,1)}, u32[]{:S(2)}, u32[]{:S(2)}) %all-to-all-start.4) | async-done | bytes 3784736 | tf_op jit(solution)/shard_map/all_to_all | solution.py:29
  222.0 3.4 %copy.41 = bf16[231,16,512]{2,1,0:T(8,128)(2,1)S(1)} copy(bf16[231,16,512]{2,0,1:T(8,128)(2,1)} %bitcast.10) | data formatting | bytes 7569408 | tf_op jit(solution)/shard_map/all_to_all | solution.py:29
  225.4 0.4 pad
  225.8 5.8 %copy.45 = bf16[29,8,16,512]{3,1,2,0:T(8,128)(2,1)} copy(bf16[29,8,16,512]{3,2,1,0:T(8,128)(2,1)S(1)} %bitcast.38) | data formatting | bytes 7602176
  231.5 0.7 copy.49
  232.2 0.7 copy.50
  (26 shorter events, 0.1 us)
Async XLA Ops:
  0.6 8.8 %copy-start = (bf16[3696,64]{0,1:T(8,128)(2,1)S(1)}, bf16[3696,64]{0,1:T(8,128)(2,1)}, u32[]{:S(2)}) copy-start(bf16[3696,64]{0,1:T(8,128)(2,1)} %param.42) | copy-start | bytes 1419268
  0.6 7.0 %copy-start.5 = (bf16[1024,64]{0,1:T(8,128)(2,1)S(1)}, bf16[1024,64]{0,1:T(8,128)(2,1)}, u32[]{:S(2)}) copy-start(bf16[1024,64]{0,1:T(8,128)(2,1)} %param.26) | copy-start | bytes 393220
  0.7 7.0 %copy-start.8 = (bf16[64,512]{1,0:T(8,128)(2,1)S(1)}, bf16[64,512]{1,0:T(8,128)(2,1)}, u32[]{:S(2)}) copy-start(bf16[64,512]{1,0:T(8,128)(2,1)} %param.25) | copy-start | bytes 196612
  2.2 7.2 %copy-start.2 = (bf16[3696,512]{1,0:T(8,128)(2,1)S(1)}, bf16[3696,512]{1,0:T(8,128)(2,1)}, u32[]{:S(2)}) copy-start(bf16[3696,512]{1,0:T(8,128)(2,1)} %param.40) | copy-start | bytes 11354116
  2.2 7.2 %copy-start.6 = (bf16[64,512]{1,0:T(8,128)(2,1)S(1)}, bf16[64,512]{1,0:T(8,128)(2,1)}, u32[]{:S(2)}) copy-start(bf16[64,512]{1,0:T(8,128)(2,1)} %param.41) | copy-start | bytes 196612
  9.4 4.3 %copy-start.3 = (bf16[3696,512]{1,0:T(8,128)(2,1)S(1)}, bf16[3696,512]{1,0:T(8,128)(2,1)}, u32[]{:S(2)}) copy-start(bf16[3696,512]{1,0:T(8,128)(2,1)} %param.44) | copy-start | bytes 11354116
  9.4 4.3 %copy-start.4 = (bf16[3696,64]{0,1:T(8,128)(2,1)S(1)}, bf16[3696,64]{0,1:T(8,128)(2,1)}, u32[]{:S(2)}) copy-start(bf16[3696,64]{0,1:T(8,128)(2,1)} %param.46) | copy-start | bytes 1419268
  9.5 4.3 %copy-start.7 = (bf16[64,512]{1,0:T(8,128)(2,1)S(1)}, bf16[64,512]{1,0:T(8,128)(2,1)}, u32[]{:S(2)}) copy-start(bf16[64,512]{1,0:T(8,128)(2,1)} %param.45) | copy-start | bytes 196612
  13.8 38.7 %copy-start.13 = (f32[128]{0:T(128)S(1)}, f32[128]{0:T(128)}, u32[]{:S(2)}) copy-start(f32[128]{0:T(128)} %param.35) | copy-start | bytes 1540
  13.8 42.9 %copy-start.14 = (f32[128]{0:T(128)S(1)}, f32[128]{0:T(128)}, u32[]{:S(2)}) copy-start(f32[128]{0:T(128)} %param.31) | copy-start | bytes 1540
  13.8 43.7 %copy-start.11 = (f32[1024]{0:T(1024)S(1)}, f32[1024]{0:T(1024)}, u32[]{:S(2)}) copy-start(f32[1024]{0:T(1024)} %param.39) | copy-start | bytes 12292
  13.8 43.7 %copy-start.12 = (f32[1024]{0:T(1024)S(1)}, f32[1024]{0:T(1024)}, u32[]{:S(2)}) copy-start(f32[1024]{0:T(1024)} %param.27) | copy-start | bytes 12292
  18.2 63.1 %copy-start.9 = (f32[3696]{0:T(1024)S(1)}, f32[3696]{0:T(1024)}, u32[]{:S(2)}) copy-start(f32[3696]{0:T(1024)} %param.47) | copy-start | bytes 44356
  18.2 63.1 %copy-start.10 = (f32[3696]{0:T(1024)S(1)}, f32[3696]{0:T(1024)}, u32[]{:S(2)}) copy-start(f32[3696]{0:T(1024)} %param.43) | copy-start | bytes 44356
  53.2 11.2 %all-to-all-start.2 = ((bf16[16,8,512]{2,1,0:T(8,128)(2,1)}), bf16[16,8,512]{2,1,0:T(8,128)(2,1)S(1)}, u32[]{:S(2)}, u32[]{:S(2)}) async-start(bf16[16,8,512]{2,1,0:T(8,128)(2,1)} %fusion.1), calls=%async_computation.2 | async-start | bytes 262144 | tf_op jit(solution)/shard_map/all_to_all | solution.py:29
  64.4 11.7 %all-to-all-start.1 = ((bf16[16,8,512]{2,1,0:T(8,128)(2,1)}), bf16[16,8,512]{2,1,0:T(8,128)(2,1)S(1)}, u32[]{:S(2)}, u32[]{:S(2)}) async-start(bf16[16,8,512]{2,1,0:T(8,128)(2,1)} %fusion), calls=%async_computation.1 | async-start | bytes 262144 | tf_op jit(solution)/shard_map/all_to_all | solution.py:29
  76.1 20.4 %all-to-all-start.3 = ((bf16[1024,8,64]{0,2,1:T(8,128)(2,1)}), bf16[1024,8,64]{0,2,1:T(8,128)(2,1)}, u32[]{:S(2)}, u32[]{:S(2)}) async-start(bf16[1024,8,64]{0,2,1:T(8,128)(2,1)} %bitcast.41), calls=%async_computation.3 | async-start | bytes 2097152 | tf_op jit(solution)/shard_map/all_to_all | solution.py:62
  96.5 21.3 %all-to-all-start = ((bf16[16,64,512]{2,1,0:T(8,128)(2,1)}), bf16[16,64,512]{2,1,0:T(8,128)(2,1)S(1)}, u32[]{:S(2)}, u32[]{:S(2)}) async-start(bf16[16,64,512]{2,1,0:T(8,128)(2,1)} %bitcast.42), calls=%async_computation | async-start | bytes 2097152 | tf_op jit(solution)/shard_map/all_to_all | solution.py:29
  117.9 52.0 %all-to-all-start.5 = ((bf16[16,231,512]{2,1,0:T(8,128)(2,1)}), bf16[16,231,512]{2,1,0:T(8,128)(2,1)}, u32[]{:S(2)}, u32[]{:S(2)}) async-start(bf16[16,231,512]{2,1,0:T(8,128)(2,1)} %all_to_all.104), calls=%async_computation.5 | async-start | bytes 7602176 | tf_op jit(solution)/shard_map/all_to_all | solution.py:29
  169.9 52.1 %all-to-all-start.4 = ((bf16[16,231,512]{2,1,0:T(8,128)(2,1)}), bf16[16,231,512]{2,1,0:T(8,128)(2,1)}, u32[]{:S(2)}, u32[]{:S(2)}) async-start(bf16[16,231,512]{2,1,0:T(8,128)(2,1)} %all_to_all.100), calls=%async_computation.4 | async-start | bytes 7602176 | tf_op jit(solution)/shard_map/all_to_all | solution.py:29
  225.8 7.1 %copy-start.1 = (bf16[3696,64]{0,1:T(8,128)(2,1)S(1)}, bf16[3696,64]{0,1:T(8,128)(2,1)}, u32[]{:S(2)}) copy-start(bf16[3696,64]{0,1:T(8,128)(2,1)} %param.42) | copy-start | bytes 1419268
where the time goes:
time: 234 us; the launch traced here: 233 us
  waiting for transfers between devices  105 us (45%)
  blocking collectives  34.2 us (15%)
  local copies, waits for them, and re-layouts  33.2 us (14%)
  starting transfers between devices  27.3 us (12%)
  other arithmetic  16.1 us (7%)
  matrix products  15.8 us (7%)
    all_to_all x5, waiting for transfers between devices, row_split(): return lax.all_to_all(merged, COL, split_axis=0, concat_axis=1, tiled=True)  91.2 us
    psum x3, blocking collectives, over_axes(): value = lax.psum(value, axis)  34.2 us
    all_to_all x5, starting transfers between devices, row_split(): return lax.all_to_all(merged, COL, split_axis=0, concat_axis=1, tiled=True)  22.2 us
    dot_general x6, matrix products, tile_merge(): jnp.dot(up, down, preferred_element_type=jnp.float32)  15.8 us
    all_to_all x5, local copies, waits for them, and re-layouts, row_split(): return lax.all_to_all(merged, COL, split_axis=0, concat_axis=1, tiled=True)  15.7 us
    unnamed x37, local copies, waits for them, and re-layouts  15.3 us
    convert_element_type x4, other arithmetic, tile_merge(): return (direction * factor[:, None]).astype(jnp.bfloat16)  14.6 us
    all_to_all x1, waiting for transfers between devices, on_device(): lax.all_to_all(o_tile, 'row', split_axis=1, concat_axis=0, tiled=True)  14 us
  transfers between devices with their start and end apart: 6, of which 6 were waited for; matrix products, arithmetic and copies ran while one was open for 12% of the time, Pallas kernels for 0%

commit v1 on v0

--- a/solution.py
+++ b/solution.py
@@ -12,7 +12,7 @@
 
 def over_axes(value, axes):
     for axis in axes:
-        value = lax.psum(value, axis)
+        value = jnp.sum(lax.all_gather(value, axis), axis=0)
     return value
 
 

time: 234 us -> 298 us (1.27)
  blocking collectives: 34.2 us -> 89.8 us
  waiting for transfers between devices: 105 us -> 85.5 us
  between operations: 0.88 us -> 16.5 us
  local copies, waits for them, and re-layouts: 33.2 us -> 40.7 us
  starting transfers between devices: 27.3 us -> 30.5 us
    all_gather x0 -> x12, blocking collectives: none -> 76.1 us  [over_axes(): value = jnp.sum(lax.all_gather(value, axis), axis=0)]
    psum x3 -> x0, blocking collectives: 34.2 us -> none  [over_axes(): value = lax.psum(value, axis)]
    all_to_all x1, waiting for transfers between devices: 14 us -> 0.01 us  [on_device(): lax.all_to_all(o_tile, 'row', split_axis=1, concat_axis=0, tiled=True)]
    unnamed x0 -> x2, blocking collectives: none -> 13.7 us
    all_to_all x5, waiting for transfers between devices: 91.2 us -> 85.5 us  [row_split(): return lax.all_to_all(merged, COL, split_axis=0, concat_axis=1, tiled=True)]
    unnamed x37 -> x64, local copies, waits for them, and re-layouts: 15.3 us -> 20.4 us
    all_to_all x5, starting transfers between devices: 22.2 us -> 25.4 us  [row_split(): return lax.all_to_all(merged, COL, split_axis=0, concat_axis=1, tiled=True)]
  transfers between devices with their start and end apart: 6 -> 7, of which waited for: 6 -> 4; matrix products, arithmetic and copies ran while one was open for 12% -> 18% of each run, Pallas kernels for 0% -> 0%
where the time goes in v1:
time: 298 us; the launch traced here: 297 us
  blocking collectives  89.8 us (30%)
  waiting for transfers between devices  85.5 us (29%)
  local copies, waits for them, and re-layouts  40.7 us (14%)
  starting transfers between devices  30.5 us (10%)
  matrix products  18 us (6%)
  between operations  16.5 us (6%)
  other arithmetic  15.7 us (5%)
    all_to_all x5, waiting for transfers between devices, row_split(): return lax.all_to_all(merged, COL, split_axis=0, concat_axis=1, tiled=True)  85.5 us
    all_gather x12, blocking collectives, over_axes(): value = jnp.sum(lax.all_gather(value, axis), axis=0)  76.1 us
    all_to_all x5, starting transfers between devices, row_split(): return lax.all_to_all(merged, COL, split_axis=0, concat_axis=1, tiled=True)  25.4 us
    unnamed x64, local copies, waits for them, and re-layouts  20.4 us
    dot_general x6, matrix products, tile_merge(): jnp.dot(up, down, preferred_element_type=jnp.float32)  18 us
    all_to_all x5, local copies, waits for them, and re-layouts, row_split(): return lax.all_to_all(merged, COL, split_axis=0, concat_axis=1, tiled=True)  15.7 us
    unnamed x2, blocking collectives  13.7 us
    convert_element_type x4, other arithmetic, tile_merge(): return (direction * factor[:, None]).astype(jnp.bfloat16)  13 us
  transfers between devices with their start and end apart: 7, of which 4 were waited for; matrix products, arithmetic and copies ran while one was open for 18% of the time, Pallas kernels for 0%

profile of v1, /device:TPU:1, one launch (start us, length us, event | category | flops | bytes accessed | tf_op | source)
XLA Modules:
  0.0 296.6 jit_solution(1188839877107082963)
XLA Ops:
  7.2 1.3 multiply_reduce_fusion.5
  8.5 8.8 %all-gather.18 = f32[4,1,128]{2,1,0:T(1,128)S(1)} all-gather(f32[1,1,128]{2,1,0:T(1,128)S(1)} %bitcast.58), channel_id=5, replica_groups=mesh['row'=8,'col_0'=4,'col_1'=2,'col_2'=2] {'col_0'}, dimensions={0}, use_global_device_ids=true | all-gather | bytes 2560 | tf_op jit(solution)/shard_map/all_gather | solution.py:15
  17.3 4.6 %all-gather.19 = f32[2,1,128]{2,1,0:T(1,128)S(1)} all-gather(f32[1,1,128]{2,1,0:T(1,128)S(1)} %bitcast.60), channel_id=6, replica_groups=mesh['row'=8,'col_0'=4,'col_1'=2,'col_2'=2] {'col_1'}, dimensions={0}, use_global_device_ids=true | all-gather | bytes 1536 | tf_op jit(solution)/shard_map/all_gather | solution.py:15
  21.9 5.3 %all-gather.20 = f32[2,1,128]{2,1,0:T(1,128)S(1)} all-gather(f32[1,1,128]{2,1,0:T(1,128)S(1)} %bitcast.61), channel_id=7, replica_groups=mesh['row'=8,'col_0'=4,'col_1'=2,'col_2'=2] {'col_2'}, dimensions={0}, use_global_device_ids=true | all-gather | bytes 1536 | tf_op jit(solution)/shard_map/all_gather | solution.py:15
  27.2 0.7 rsqrt_multiply_fusion.5
  27.9 0.7 fusion
  28.6 4.9 %all-to-all-start.1 = ((bf16[16,8,512]{2,1,0:T(8,128)(2,1)}), bf16[16,8,512]{2,1,0:T(8,128)(2,1)S(1)}, u32[]{:S(2)}, u32[]{:S(2)}) async-start(bf16[16,8,512]{2,1,0:T(8,128)(2,1)} %fusion), calls=%async_computation.1 | async-start | bytes 262144 | tf_op jit(solution)/shard_map/all_to_all | solution.py:29
  33.6 1.2 dynamic-slice
  35.5 6.4 %multiply_reduce_fusion.1 = (f32[3696]{0:T(1024)S(1)}, f32[3696,512]{1,0:T(8,128)}) fusion(bf16[3696,64]{0,1:T(8,128)(2,1)S(1)} %copy-done, bf16[64,512]{1,0:T(8,128)(2,1)} %param.41, bf16[3696,512]{1,0:T(8,128)(2,1)} %param.40), kind=kOutput, calls=%fused_computation.4 | convolution fusion | flops 249786768 | bytes 11907520 | tf_op jit(solution)/shard_map/dot_general | solution.py:20
  42.5 6.5 %multiply_reduce_fusion = (f32[3696]{0:T(1024)S(1)}, f32[3696,512]{1,0:T(8,128)}) fusion(bf16[3696,64]{0,1:T(8,128)(2,1)S(1)} %copy-done.3, bf16[64,512]{1,0:T(8,128)(2,1)S(1)} %copy-done.9, bf16[3696,512]{1,0:T(8,128)(2,1)} %param.44), kind=kOutput, calls=%fused_computation.1 | convolution fusion | flops 249786768 | bytes 11907520 | tf_op jit(solution)/shard_map/dot_general | solution.py:20
  50.1 1.3 copy.49
  51.4 1.7 multiply_reduce_fusion.2
  53.2 9.7 %all-gather.9 = f32[4096]{0:T(1024)S(1)} all-gather(f32[1024]{0:T(1024)S(1)} %get-tuple-element.18), channel_id=11, replica_groups=mesh['row'=8,'col_0'=4,'col_1'=2,'col_2'=2] {'col_0'}, dimensions={0}, use_global_device_ids=true | all-gather | bytes 20480 | tf_op jit(solution)/shard_map/all_gather | solution.py:15
  62.9 4.7 %all-gather.10 = f32[2048]{0:T(1024)S(1)} all-gather(f32[1024]{0:T(1024)S(1)} %reduce_sum.229), channel_id=12, replica_groups=mesh['row'=8,'col_0'=4,'col_1'=2,'col_2'=2] {'col_1'}, dimensions={0}, use_global_device_ids=true | all-gather | bytes 12288 | tf_op jit(solution)/shard_map/all_gather | solution.py:15
  67.7 5.9 %all-gather.11 = f32[2048]{0:T(1024)S(1)} all-gather(f32[1024]{0:T(1024)S(1)} %reduce_sum.230), channel_id=13, replica_groups=mesh['row'=8,'col_0'=4,'col_1'=2,'col_2'=2] {'col_2'}, dimensions={0}, use_global_device_ids=true | all-gather | bytes 12288 | tf_op jit(solution)/shard_map/all_gather | solution.py:15
  73.9 7.2 %all-gather.21 = f32[4,1,128]{2,1,0:T(1,128)S(1)} all-gather(f32[1,1,128]{2,1,0:T(1,128)S(1)} %bitcast.59), channel_id=8, replica_groups=mesh['row'=8,'col_0'=4,'col_1'=2,'col_2'=2] {'col_0'}, dimensions={0}, use_global_device_ids=true | all-gather | bytes 2560 | tf_op jit(solution)/shard_map/all_gather | solution.py:15
  81.1 4.6 %all-gather.22 = f32[2,1,128]{2,1,0:T(1,128)S(1)} all-gather(f32[1,1,128]{2,1,0:T(1,128)S(1)} %bitcast.62), channel_id=9, replica_groups=mesh['row'=8,'col_0'=4,'col_1'=2,'col_2'=2] {'col_1'}, dimensions={0}, use_global_device_ids=true | all-gather | bytes 1536 | tf_op jit(solution)/shard_map/all_gather | solution.py:15
  85.7 5.0 %all-gather.23 = f32[2,1,128]{2,1,0:T(1,128)S(1)} all-gather(f32[1,1,128]{2,1,0:T(1,128)S(1)} %bitcast.63), channel_id=10, replica_groups=mesh['row'=8,'col_0'=4,'col_1'=2,'col_2'=2] {'col_2'}, dimensions={0}, use_global_device_ids=true | all-gather | bytes 1536 | tf_op jit(solution)/shard_map/all_gather | solution.py:15
  90.7 0.7 fusion.1
  91.5 4.9 %all-to-all-start.2 = ((bf16[16,8,512]{2,1,0:T(8,128)(2,1)}), bf16[16,8,512]{2,1,0:T(8,128)(2,1)S(1)}, u32[]{:S(2)}, u32[]{:S(2)}) async-start(bf16[16,8,512]{2,1,0:T(8,128)(2,1)} %fusion.1), calls=%async_computation.2 | async-start | bytes 262144 | tf_op jit(solution)/shard_map/all_to_all | solution.py:29
  96.4 1.2 multiply_convert_fusion.2
  97.7 6.4 %all-to-all-done.2 = bf16[16,8,512]{2,1,0:T(8,128)(2,1)S(1)} async-done(((bf16[16,8,512]{2,1,0:T(8,128)(2,1)}), bf16[16,8,512]{2,1,0:T(8,128)(2,1)S(1)}, u32[]{:S(2)}, u32[]{:S(2)}) %all-to-all-start.2) | async-done | bytes 131104 | tf_op jit(solution)/shard_map/all_to_all | solution.py:29
  104.0 5.1 %all-to-all-start.3 = ((bf16[1024,8,64]{0,2,1:T(8,128)(2,1)}), bf16[1024,8,64]{0,2,1:T(8,128)(2,1)}, u32[]{:S(2)}, u32[]{:S(2)}) async-start(bf16[1024,8,64]{0,2,1:T(8,128)(2,1)} %bitcast.49), calls=%async_computation.3 | async-start | bytes 2097152 | tf_op jit(solution)/shard_map/all_to_all | solution.py:62
  109.2 1.8 multiply_reduce_fusion.3
  110.9 10.1 %all-gather = f32[4096]{0:T(1024)S(1)} all-gather(f32[1024]{0:T(1024)S(1)} %get-tuple-element.12), channel_id=2, replica_groups=mesh['row'=8,'col_0'=4,'col_1'=2,'col_2'=2] {'col_0'}, dimensions={0}, use_global_device_ids=true | all-gather | bytes 20480 | tf_op jit(solution)/shard_map/all_gather | solution.py:15
  121.1 4.7 %all-gather.1 = f32[2048]{0:T(1024)S(1)} all-gather(f32[1024]{0:T(1024)S(1)} %reduce_sum.217), channel_id=3, replica_groups=mesh['row'=8,'col_0'=4,'col_1'=2,'col_2'=2] {'col_1'}, dimensions={0}, use_global_device_ids=true | all-gather | bytes 12288 | tf_op jit(solution)/shard_map/all_gather | solution.py:15
  125.8 5.5 %all-gather.2 = f32[2048]{0:T(1024)S(1)} all-gather(f32[1024]{0:T(1024)S(1)} %reduce_sum.218), channel_id=4, replica_groups=mesh['row'=8,'col_0'=4,'col_1'=2,'col_2'=2] {'col_2'}, dimensions={0}, use_global_device_ids=true | all-gather | bytes 12288 | tf_op jit(solution)/shard_map/all_gather | solution.py:15
  131.3 1.2 multiply_convert_fusion.3
  135.0 0.9 reshape.48
  136.0 0.9 reshape.51
  137.8 7.8 %all-reduce.8 = (f32[7392]{0:T(1024)S(1)}, f32[7392]{0:T(1024)S(1)}) all-reduce(f32[7392]{0:T(1024)S(1)} %dynamic-update-slice.1, f32[7392]{0:T(1024)S(1)} %dynamic-update-slice.4), channel_id=15, replica_groups=mesh['row'=8,'col_0'=4,'col_1'=2,'col_2'=2] {'col_1'}, use_global_device_ids=true, to_apply=%add.1 | all-reduce | flops 14784 | bytes 118272
  146.7 5.9 %all-reduce.7 = (f32[7392]{0:T(1024)S(1)}, f32[7392]{0:T(1024)S(1)}) all-reduce(f32[7392]{0:T(1024)S(1)} %dynamic-update-slice.2, f32[7392]{0:T(1024)S(1)} %dynamic-update-slice.5), channel_id=16, replica_groups=mesh['row'=8,'col_0'=4,'col_1'=2,'col_2'=2] {'col_2'}, use_global_device_ids=true, to_apply=%add.2 | all-reduce | flops 14784 | bytes 118272
  152.7 4.9 %all-to-all-start = ((bf16[16,64,512]{2,1,0:T(8,128)(2,1)}), bf16[16,64,512]{2,1,0:T(8,128)(2,1)S(1)}, u32[]{:S(2)}, u32[]{:S(2)}) async-start(bf16[16,64,512]{2,1,0:T(8,128)(2,1)} %bitcast.50), calls=%async_computation | async-start | bytes 2097152 | tf_op jit(solution)/shard_map/all_to_all | solution.py:29
  157.7 5.3 %multiply_convert_fusion = bf16[3696,512]{1,0:T(8,128)(2,1)} fusion(f32[3696,512]{1,0:T(8,128)} %get-tuple-element.23, f32[3696]{0:T(1024)S(1)} %rsqrt_multiply_fusion), kind=kLoop, calls=%fused_computation | loop fusion | flops 3784704 | bytes 11368896 | tf_op jit(solution)/shard_map/convert_element_type | solution.py:24
  163.0 4.0 %all_to_all.104 = bf16[16,231,512]{2,1,0:T(8,128)(2,1)} reshape(bf16[3696,512]{1,0:T(8,128)(2,1)} %multiply_convert_fusion) | data formatting | bytes 7569408 | tf_op jit(solution)/shard_map/all_to_all | solution.py:29
  166.9 7.8 %all-to-all-done = bf16[16,64,512]{2,1,0:T(8,128)(2,1)S(1)} async-done(((bf16[16,64,512]{2,1,0:T(8,128)(2,1)}), bf16[16,64,512]{2,1,0:T(8,128)(2,1)S(1)}, u32[]{:S(2)}, u32[]{:S(2)}) %all-to-all-start) | async-done | bytes 1048608 | tf_op jit(solution)/shard_map/all_to_all | solution.py:29
  174.8 5.3 %all-to-all-start.5 = ((bf16[16,231,512]{2,1,0:T(8,128)(2,1)}), bf16[16,231,512]{2,1,0:T(8,128)(2,1)}, u32[]{:S(2)}, u32[]{:S(2)}) async-start(bf16[16,231,512]{2,1,0:T(8,128)(2,1)} %all_to_all.104), calls=%async_computation.5 | async-start | bytes 7602176 | tf_op jit(solution)/shard_map/all_to_all | solution.py:29
  180.2 5.3 %multiply_convert_fusion.1 = bf16[3696,512]{1,0:T(8,128)(2,1)} fusion(f32[3696,512]{1,0:T(8,128)} %get-tuple-element.21, f32[3696]{0:T(1024)S(1)} %rsqrt_multiply_fusion.1), kind=kLoop, calls=%fused_computation.3 | loop fusion | flops 3784704 | bytes 11368896 | tf_op jit(solution)/shard_map/convert_element_type | solution.py:24
  185.5 4.0 %all_to_all.100 = bf16[16,231,512]{2,1,0:T(8,128)(2,1)} reshape(bf16[3696,512]{1,0:T(8,128)(2,1)} %multiply_convert_fusion.1) | data formatting | bytes 7569408 | tf_op jit(solution)/shard_map/all_to_all | solution.py:29
  189.5 37.4 %all-to-all-done.5 = bf16[16,231,512]{2,1,0:T(8,128)(2,1)} async-done(((bf16[16,231,512]{2,1,0:T(8,128)(2,1)}), bf16[16,231,512]{2,1,0:T(8,128)(2,1)}, u32[]{:S(2)}, u32[]{:S(2)}) %all-to-all-start.5) | async-done | bytes 3784736 | tf_op jit(solution)/shard_map/all_to_all | solution.py:29
  226.8 5.3 %all-to-all-start.4 = ((bf16[16,231,512]{2,1,0:T(8,128)(2,1)}), bf16[16,231,512]{2,1,0:T(8,128)(2,1)}, u32[]{:S(2)}, u32[]{:S(2)}) async-start(bf16[16,231,512]{2,1,0:T(8,128)(2,1)} %all_to_all.100), calls=%async_computation.4 | async-start | bytes 7602176 | tf_op jit(solution)/shard_map/all_to_all | solution.py:29
  232.1 2.3 copy.54
  234.4 1.1 copy.53
  235.5 3.4 %copy.52 = bf16[231,16,512]{2,1,0:T(8,128)(2,1)S(1)} copy(bf16[231,16,512]{2,0,1:T(8,128)(2,1)} %bitcast.20) | data formatting | bytes 7569408 | tf_op jit(solution)/shard_map/all_to_all | solution.py:29
  239.2 5.8 %copy.56 = bf16[29,8,16,512]{3,1,2,0:T(8,128)(2,1)} copy(bf16[29,8,16,512]{3,2,1,0:T(8,128)(2,1)S(1)} %bitcast.48) | data formatting | bytes 7602176
  245.0 33.9 %all-to-all-done.4 = bf16[16,231,512]{2,1,0:T(8,128)(2,1)} async-done(((bf16[16,231,512]{2,1,0:T(8,128)(2,1)}), bf16[16,231,512]{2,1,0:T(8,128)(2,1)}, u32[]{:S(2)}, u32[]{:S(2)}) %all-to-all-start.4) | async-done | bytes 3784736 | tf_op jit(solution)/shard_map/all_to_all | solution.py:29
  278.9 3.4 %copy.51 = bf16[231,16,512]{2,1,0:T(8,128)(2,1)S(1)} copy(bf16[231,16,512]{2,0,1:T(8,128)(2,1)} %bitcast.19) | data formatting | bytes 7569408 | tf_op jit(solution)/shard_map/all_to_all | solution.py:29
  282.7 5.8 %copy.55 = bf16[29,8,16,512]{3,1,2,0:T(8,128)(2,1)} copy(bf16[29,8,16,512]{3,2,1,0:T(8,128)(2,1)S(1)} %bitcast.47) | data formatting | bytes 7602176
  (99 shorter events, 7.6 us)
Async XLA Ops:
  7.2 28.3 %copy-start = (bf16[3696,64]{0,1:T(8,128)(2,1)S(1)}, bf16[3696,64]{0,1:T(8,128)(2,1)}, u32[]{:S(2)}) copy-start(bf16[3696,64]{0,1:T(8,128)(2,1)} %param.42) | copy-start | bytes 1419268
  28.6 62.9 %all-to-all-start.1 = ((bf16[16,8,512]{2,1,0:T(8,128)(2,1)}), bf16[16,8,512]{2,1,0:T(8,128)(2,1)S(1)}, u32[]{:S(2)}, u32[]{:S(2)}) async-start(bf16[16,8,512]{2,1,0:T(8,128)(2,1)} %fusion), calls=%async_computation.1 | async-start | bytes 262144 | tf_op jit(solution)/shard_map/all_to_all | solution.py:29
  33.6 101.5 %all-reduce.11.cloned.1.call-start = ((), (), s32[]{:S(2)}) async-start(), calls=%async_computation.6 | async-start | bytes 245760
  35.5 6.9 %copy-start.3 = (bf16[3696,64]{0,1:T(8,128)(2,1)S(1)}, bf16[3696,64]{0,1:T(8,128)(2,1)}, u32[]{:S(2)}) copy-start(bf16[3696,64]{0,1:T(8,128)(2,1)} %param.46) | copy-start | bytes 1419268
  35.5 6.9 %copy-start.9 = (bf16[64,512]{1,0:T(8,128)(2,1)S(1)}, bf16[64,512]{1,0:T(8,128)(2,1)}, u32[]{:S(2)}) copy-start(bf16[64,512]{1,0:T(8,128)(2,1)} %param.45) | copy-start | bytes 196612
  42.4 6.6 %copy-start.5 = (f32[14784]{0:T(1024)}, f32[14784]{0:T(1024)S(1)}, u32[]{:S(2)}) copy-start(f32[14784]{0:T(1024)S(1)} %dynamic-update-slice) | copy-start | bytes 177412
  42.4 7.7 %copy-start.2 = (bf16[1024,512]{1,0:T(8,128)(2,1)S(1)}, bf16[1024,512]{1,0:T(8,128)(2,1)}, u32[]{:S(2)}) copy-start(bf16[1024,512]{1,0:T(8,128)(2,1)} %param.36) | copy-start | bytes 3145732
  42.4 9.0 %copy-start.6 = (bf16[1024,64]{0,1:T(8,128)(2,1)S(1)}, bf16[1024,64]{0,1:T(8,128)(2,1)}, u32[]{:S(2)}) copy-start(bf16[1024,64]{0,1:T(8,128)(2,1)} %param.38) | copy-start | bytes 393220
  42.4 9.0 %copy-start.10 = (bf16[64,512]{1,0:T(8,128)(2,1)S(1)}, bf16[64,512]{1,0:T(8,128)(2,1)}, u32[]{:S(2)}) copy-start(bf16[64,512]{1,0:T(8,128)(2,1)} %param.37) | copy-start | bytes 196612
  49.0 24.6 %copy-start.7 = (bf16[128,512]{1,0:T(8,128)(2,1)S(1)}, bf16[128,512]{1,0:T(8,128)(2,1)}, u32[]{:S(2)}) copy-start(bf16[128,512]{1,0:T(8,128)(2,1)} %param.32) | copy-start | bytes 393220
  49.0 24.6 %copy-start.12 = (bf16[64,512]{1,0:T(8,128)(2,1)S(1)}, bf16[64,512]{1,0:T(8,128)(2,1)}, u32[]{:S(2)}) copy-start(bf16[64,512]{1,0:T(8,128)(2,1)} %param.33) | copy-start | bytes 196612
  49.0 24.6 %copy-start.13 = (bf16[128,64]{0,1:T(8,128)(2,1)S(1)}, bf16[128,64]{0,1:T(8,128)(2,1)}, u32[]{:S(2)}) copy-start(bf16[128,64]{0,1:T(8,128)(2,1)} %param.34) | copy-start | bytes 49156
  49.0 41.8 %copy-start.18 = (f32[128]{0:T(128)S(1)}, f32[128]{0:T(128)}, u32[]{:S(2)}) copy-start(f32[128]{0:T(128)} %param.35) | copy-start | bytes 1540
  49.0 42.5 %copy-start.16 = (f32[1024]{0:T(1024)S(1)}, f32[1024]{0:T(1024)}, u32[]{:S(2)}) copy-start(f32[1024]{0:T(1024)} %param.39) | copy-start | bytes 12292
  49.4 0.6 copy-start.4
  53.1 56.0 %copy-start.8 = (bf16[1024,64]{0,1:T(8,128)(2,1)S(1)}, bf16[1024,64]{0,1:T(8,128)(2,1)}, u32[]{:S(2)}) copy-start(bf16[1024,64]{0,1:T(8,128)(2,1)} %param.26) | copy-start | bytes 393220
  53.1 56.0 %copy-start.11 = (bf16[64,512]{1,0:T(8,128)(2,1)S(1)}, bf16[64,512]{1,0:T(8,128)(2,1)}, u32[]{:S(2)}) copy-start(bf16[64,512]{1,0:T(8,128)(2,1)} %param.25) | copy-start | bytes 196612
  91.5 12.5 %all-to-all-start.2 = ((bf16[16,8,512]{2,1,0:T(8,128)(2,1)}), bf16[16,8,512]{2,1,0:T(8,128)(2,1)S(1)}, u32[]{:S(2)}, u32[]{:S(2)}) async-start(bf16[16,8,512]{2,1,0:T(8,128)(2,1)} %fusion.1), calls=%async_computation.2 | async-start | bytes 262144 | tf_op jit(solution)/shard_map/all_to_all | solution.py:29
  96.4 34.9 %copy-start.17 = (f32[1024]{0:T(1024)S(1)}, f32[1024]{0:T(1024)}, u32[]{:S(2)}) copy-start(f32[1024]{0:T(1024)} %param.27) | copy-start | bytes 12292
  104.0 48.7 %all-to-all-start.3 = ((bf16[1024,8,64]{0,2,1:T(8,128)(2,1)}), bf16[1024,8,64]{0,2,1:T(8,128)(2,1)}, u32[]{:S(2)}, u32[]{:S(2)}) async-start(bf16[1024,8,64]{0,2,1:T(8,128)(2,1)} %bitcast.49), calls=%async_computation.3 | async-start | bytes 2097152 | tf_op jit(solution)/shard_map/all_to_all | solution.py:62
  109.1 23.4 %copy-start.20 = (u32[128]{0:T(128)S(1)}, u32[128]{0:T(128)}, u32[]{:S(2)}) copy-start(u32[128]{0:T(128)} %constant.13) | copy-start | bytes 1540
  109.1 24.6 %copy-start.19 = (u32[128]{0:T(128)S(1)}, u32[128]{0:T(128)}, u32[]{:S(2)}) copy-start(u32[128]{0:T(128)} %constant.18) | copy-start | bytes 1540
  109.1 43.6 %copy-start.14 = (f32[3696]{0:T(1024)S(1)}, f32[3696]{0:T(1024)}, u32[]{:S(2)}) copy-start(f32[3696]{0:T(1024)} %param.47) | copy-start | bytes 44356
  152.7 22.0 %all-to-all-start = ((bf16[16,64,512]{2,1,0:T(8,128)(2,1)}), bf16[16,64,512]{2,1,0:T(8,128)(2,1)S(1)}, u32[]{:S(2)}, u32[]{:S(2)}) async-start(bf16[16,64,512]{2,1,0:T(8,128)(2,1)} %bitcast.50), calls=%async_computation | async-start | bytes 2097152 | tf_op jit(solution)/shard_map/all_to_all | solution.py:29
  166.9 13.3 %copy-start.15 = (f32[3696]{0:T(1024)S(1)}, f32[3696]{0:T(1024)}, u32[]{:S(2)}) copy-start(f32[3696]{0:T(1024)} %param.43) | copy-start | bytes 44356
  174.8 52.1 %all-to-all-start.5 = ((bf16[16,231,512]{2,1,0:T(8,128)(2,1)}), bf16[16,231,512]{2,1,0:T(8,128)(2,1)}, u32[]{:S(2)}, u32[]{:S(2)}) async-start(bf16[16,231,512]{2,1,0:T(8,128)(2,1)} %all_to_all.104), calls=%async_computation.5 | async-start | bytes 7602176 | tf_op jit(solution)/shard_map/all_to_all | solution.py:29
  226.8 52.1 %all-to-all-start.4 = ((bf16[16,231,512]{2,1,0:T(8,128)(2,1)}), bf16[16,231,512]{2,1,0:T(8,128)(2,1)}, u32[]{:S(2)}, u32[]{:S(2)}) async-start(bf16[16,231,512]{2,1,0:T(8,128)(2,1)} %all_to_all.100), calls=%async_computation.4 | async-start | bytes 7602176 | tf_op jit(solution)/shard_map/all_to_all | solution.py:29
  282.7 7.1 %copy-start.1 = (bf16[3696,64]{0,1:T(8,128)(2,1)S(1)}, bf16[3696,64]{0,1:T(8,128)(2,1)}, u32[]{:S(2)}) copy-start(bf16[3696,64]{0,1:T(8,128)(2,1)} %param.42) | copy-start | bytes 1419268
Sparse Core Ops, SparseCore 0:
  50.2 41.3 all-reduce.10
